TPU v7x, 32 devices: a whole 2x2x4 slice. The times are simulated.
32 devices in a mesh: seq: 16 (over z, y, core), res: 2 (over x).
Axes of the slice: x: 2, y: 2, z: 4, core: 2. Of those that a mesh axis runs over, the one named last changes fastest.
Arguments:
- homolog_embedding: bfloat16 [256, 128, 256], P('seq', 'res'), may hold values from -6 to 6
- pair_features: bfloat16 [128, 128, 128], P('seq', 'res'), may hold values from -6 to 6
- row_present_mask: int32 [256], replicated, may hold values 0 or 1
- residue_keep_mask: int32 [128], replicated, may hold values 0 or 1
- query_weight: bfloat16 [256, 256], replicated, may hold values from -64 to 64
- key_weight: bfloat16 [256, 256], replicated, may hold values from -1 to 1
- content_matrix: bfloat16 [256, 256], replicated, may hold values from -0.375 to 0.375
- sigmoid_switch_matrix: bfloat16 [256, 256], replicated, may hold values from -0.375 to 0.375
- focus_merge_matrix: bfloat16 [256, 256], replicated, may hold values from -0.375 to 0.375
- widening_matrix: bfloat16 [256, 1024], replicated, may hold values from -0.375 to 0.375
- narrowing_matrix: bfloat16 [1024, 256], replicated, may hold values from -0.1875 to 0.1875
- first_factor_matrix: bfloat16 [256, 32], replicated, may hold values from -0.375 to 0.375
- second_factor_matrix: bfloat16 [256, 32], replicated, may hold values from -0.375 to 0.375
- outer_product_weight: bfloat16 [1024, 128], replicated, may hold values from -1 to 1
- outer_product_bias: float32 [128], replicated, may hold values from -3 to 3
- pair_up_weight: bfloat16 [128, 512], replicated, may hold values from -0.5 to 0.5
- pair_down_weight: bfloat16 [512, 128], replicated, may hold values from -0.25 to 0.25
Outputs:
- msa_update: bfloat16 [256, 128, 256], P('seq', 'res')
- pair_update: bfloat16 [128, 128, 128], P('seq', 'res')
All inputs are finite; a program needn't handle non-finite values.
Results may differ from a plain program's by a relative error of at most 0.012.
Values may be sent and summed in bfloat16 or wider, within the bound.
A program may use at most 64 MiB of HBM per device.

v0:
```python
import math

import jax
import jax.numpy as jnp
from jax import lax
from jax.sharding import PartitionSpec as P

FOCUS_NUMBER = 8
FOCUS_BREADTH = 32
COUPLING_DIM = 32


epsilon = 1e-05
mask_fill = 1000000000.0


def layer_norm(values):
    centre = values - jnp.mean(values, axis=-1, keepdims=True)
    spread = jnp.mean(centre * centre, axis=-1, keepdims=True)
    return centre * lax.rsqrt(spread + epsilon)


def column_delta(block, row_present_flags, attention_weights):
    (
        query_weight,
        key_weight,
        content_matrix,
        sigmoid_switch_matrix,
        focus_merge_matrix,
        widening_matrix,
        narrowing_matrix,
        first_factor_matrix,
        second_factor_matrix,
    ) = attention_weights
    row_count, item_count, channel_width = block.shape
    inputs = block.astype(jnp.float32)
    normed = layer_norm(inputs).astype(jnp.bfloat16)
    scaling = 1.0 / math.sqrt(FOCUS_BREADTH)
    queries = (jnp.dot(normed, query_weight, preferred_element_type=jnp.float32) * scaling).astype(
        jnp.bfloat16
    )
    queries = queries.reshape(row_count, item_count, FOCUS_NUMBER, FOCUS_BREADTH)
    keys_all = jnp.dot(normed, key_weight, preferred_element_type=jnp.float32).astype(jnp.bfloat16)
    keys_all = keys_all.reshape(row_count, item_count, FOCUS_NUMBER, FOCUS_BREADTH)
    values_all = jnp.dot(normed, content_matrix, preferred_element_type=jnp.float32).astype(
        jnp.bfloat16
    )
    values_all = values_all.reshape(row_count, item_count, FOCUS_NUMBER, FOCUS_BREADTH)
    gate_values = jax.nn.sigmoid(
        jnp.dot(normed, sigmoid_switch_matrix, preferred_element_type=jnp.float32)
    )
    scores = jnp.einsum("skhd,tkhd->khst", queries, keys_all, preferred_element_type=jnp.float32)
    scores = scores + ((row_present_flags - 1.0) * mask_fill)[None, None, None, :]
    peak_score = jnp.max(scores, axis=-1, keepdims=True)
    exponent = jnp.exp(scores - peak_score)
    probs = (exponent / jnp.sum(exponent, axis=-1, keepdims=True)).astype(jnp.bfloat16)
    attended = jnp.einsum("khst,tkhd->skhd", probs, values_all, preferred_element_type=jnp.float32)
    attended = attended.reshape(row_count, item_count, FOCUS_NUMBER * FOCUS_BREADTH)
    gated = (gate_values * attended).astype(jnp.bfloat16)
    after_attn = (
        inputs + jnp.dot(gated, focus_merge_matrix, preferred_element_type=jnp.float32)
    ).astype(jnp.bfloat16)
    normed_two = layer_norm(after_attn.astype(jnp.float32)).astype(jnp.bfloat16)
    hidden = jax.nn.relu(
        jnp.dot(normed_two, widening_matrix, preferred_element_type=jnp.float32)
    ).astype(jnp.bfloat16)
    after_trans = (
        after_attn.astype(jnp.float32)
        + jnp.dot(hidden, narrowing_matrix, preferred_element_type=jnp.float32)
    ).astype(jnp.bfloat16)
    normed_three = layer_norm(after_trans.astype(jnp.float32)).astype(jnp.bfloat16)
    row_scale = row_present_flags[:, None, None]
    left_proj = (
        jnp.dot(normed_three, first_factor_matrix, preferred_element_type=jnp.float32) * row_scale
    ).astype(jnp.bfloat16)
    right_proj = (
        jnp.dot(normed_three, second_factor_matrix, preferred_element_type=jnp.float32) * row_scale
    ).astype(jnp.bfloat16)
    return (after_trans, left_proj, right_proj)


def pair_block_update(
    left_rows,
    right_full,
    pair_block,
    norm_block,
    outer_product_weight,
    outer_product_bias,
    pair_up_weight,
    pair_down_weight,
):
    outer = jnp.einsum(
        "sic,sje->ijce", left_rows, right_full, preferred_element_type=jnp.float32
    ).astype(jnp.bfloat16)
    row_span, column_extent = norm_block.shape
    flat = outer.reshape(row_span, column_extent, COUPLING_DIM * COUPLING_DIM)
    projected = (
        jnp.dot(flat, outer_product_weight, preferred_element_type=jnp.float32) + outer_product_bias
    )
    outer_mean = projected / jnp.maximum(norm_block, 1.0)[:, :, None]
    pair_mid = (pair_block.astype(jnp.float32) + outer_mean).astype(jnp.bfloat16)
    normed = layer_norm(pair_mid.astype(jnp.float32)).astype(jnp.bfloat16)
    hidden = jax.nn.relu(
        jnp.dot(normed, pair_up_weight, preferred_element_type=jnp.float32)
    ).astype(jnp.bfloat16)
    return (
        pair_mid.astype(jnp.float32)
        + jnp.dot(hidden, pair_down_weight, preferred_element_type=jnp.float32)
    ).astype(jnp.bfloat16)


def per_device(
    homolog_embedding,
    pair_features,
    row_present_mask,
    residue_keep_mask,
    query_weight,
    key_weight,
    content_matrix,
    sigmoid_switch_matrix,
    focus_merge_matrix,
    widening_matrix,
    narrowing_matrix,
    first_factor_matrix,
    second_factor_matrix,
    outer_product_weight,
    outer_product_bias,
    pair_up_weight,
    pair_down_weight,
):
    seq_count = lax.axis_size("seq")
    res_count = lax.axis_size("res")
    seq_index = lax.axis_index("seq")
    res_index = lax.axis_index("res")
    shard_rows, column_extent, channel_width = homolog_embedding.shape
    residue_total = column_extent * res_count
    row_span = residue_total // seq_count
    owned_columns = column_extent // seq_count
    row_present_flags = row_present_mask.astype(jnp.float32)
    attention_weights = (
        query_weight,
        key_weight,
        content_matrix,
        sigmoid_switch_matrix,
        focus_merge_matrix,
        widening_matrix,
        narrowing_matrix,
        first_factor_matrix,
        second_factor_matrix,
    )
    grouped = homolog_embedding.reshape(shard_rows, seq_count, owned_columns, channel_width)
    flat_block = lax.all_to_all(grouped, "seq", split_axis=1, concat_axis=0, tiled=True)[:, 0]
    after_trans, left_proj, right_proj = column_delta(
        flat_block, row_present_flags, attention_weights
    )
    alignment_columns = after_trans[:, None]
    left_column_set = left_proj[:, None]
    right_column_set = right_proj[:, None]
    alignment_columns = alignment_columns[:, 0]
    left_column_set = left_column_set[:, 0]
    right_column_set = right_column_set[:, 0]
    alignment_output, left_home = (
        lax.all_to_all(alignment_columns, "seq", split_axis=0, concat_axis=1, tiled=True),
        lax.all_to_all(left_column_set, "seq", split_axis=0, concat_axis=1, tiled=True),
    )
    right_full = lax.all_gather(right_column_set, "seq", axis=1, tiled=True)
    left_wide = lax.all_gather(left_home, "res", axis=1, tiled=True)
    left_rows = lax.all_to_all(left_wide, "seq", split_axis=1, concat_axis=0, tiled=True)
    row_res = lax.dynamic_slice_in_dim(residue_keep_mask, seq_index * row_span, row_span, 0)
    col_res = lax.dynamic_slice_in_dim(
        residue_keep_mask, res_index * column_extent, column_extent, 0
    )
    left_rows = left_rows * row_res.astype(jnp.bfloat16)[None, :, None]
    right_full = right_full * col_res.astype(jnp.bfloat16)[None, :, None]
    live_rows = jnp.sum(row_present_flags)
    norm_tile = (
        live_rows * row_res.astype(jnp.float32)[:, None] * col_res.astype(jnp.float32)[None, :]
    )
    overall_rows = left_rows.shape[0]
    block_rows = math.gcd(row_span, 8)
    block_count = row_span // block_rows
    left_groups = left_rows.reshape(overall_rows, block_count, block_rows, COUPLING_DIM).transpose(
        1, 0, 2, 3
    )
    pair_groups = pair_features.reshape(
        block_count, block_rows, column_extent, pair_features.shape[2]
    )
    norm_groups = norm_tile.reshape(block_count, block_rows, column_extent)

    def per_rows(pieces):
        left_block, pair_block, norm_block = pieces
        return pair_block_update(
            left_block,
            right_full,
            pair_block,
            norm_block,
            outer_product_weight,
            outer_product_bias,
            pair_up_weight,
            pair_down_weight,
        )

    pair_output = lax.map(per_rows, (left_groups, pair_groups, norm_groups))
    pair_output = pair_output.reshape(row_span, column_extent, pair_features.shape[2])
    return (alignment_output, pair_output)


def solution(mesh):
    placed = (
        P("seq", "res", None),
        P("seq", "res", None),
        P(),
        P(),
        P(),
        P(),
        P(),
        P(),
        P(),
        P(),
        P(),
        P(),
        P(),
        P(),
        P(),
        P(),
        P(),
    )
    return jax.shard_map(
        per_device,
        mesh=mesh,
        in_specs=placed,
        out_specs=(P("seq", "res", None), P("seq", "res", None)),
        check_vma=False,
    )
```

profile of v0, /device:TPU:15, one launch (start us, length us, event | category | flops | bytes accessed | tf_op | source)
XLA Modules:
  0.0 127.8 jit_solution(13391735593208518622)
XLA Ops:
  7.2 0.0 copy-start
  7.2 2.2 %copy.150 = bf16[16,64,256]{2,0,1:T(8,128)(2,1)} copy(bf16[16,64,256]{2,1,0:T(8,128)(2,1)} %param.17) | data formatting | bytes 1048576 | tf_op args[0]
  9.4 6.5 %all-to-all-start = ((bf16[16,16,4,256]{3,0,2,1:T(8,128)(2,1)}), bf16[16,16,4,256]{3,0,2,1:T(8,128)(2,1)S(1)}, u32[]{:S(2)}, u32[]{:S(2)}) async-start(bf16[16,16,4,256]{3,0,2,1:T(8,128)(2,1)} %bitcast), calls=%async_computation | async-start | bytes 1048576 | tf_op jit(solution)/shard_map/all_to_all | solution.py:152
  15.9 0.0 all-gather.2.cloned.1.call-start
  15.9 0.7 convert_element_type.120
  16.6 1.3 %convert_reduce_fusion.2 = (f32[]{:T(128)}, f32[256]{0:T(256)S(1)}) fusion(s32[256]{0:T(256)} %param.19), kind=kLoop, calls=%fused_computation.96 | loop fusion | flops 1023 | bytes 2052 | tf_op jit(solution)/shard_map/reduce_sum | solution.py:175
  17.9 11.5 %all-to-all-done = bf16[16,16,4,256]{3,0,2,1:T(8,128)(2,1)S(1)} async-done(((bf16[16,16,4,256]{3,0,2,1:T(8,128)(2,1)}), bf16[16,16,4,256]{3,0,2,1:T(8,128)(2,1)S(1)}, u32[]{:S(2)}, u32[]{:S(2)}) %all-to-all-start) | async-done | bytes 524320 | tf_op jit(solution)/shard_map/all_to_all | solution.py:152
  29.5 0.2 fusion.39
  29.7 0.0 copy-start.1
  29.7 0.1 div.52
  29.8 0.4 multiply_reduce_fusion
  30.3 0.1 rsqrt.37
  30.4 0.1 convert_bitcast_fusion.1
  30.5 0.0 copy-start.3
  30.5 0.1 copy.151
  30.6 0.3 copy.161
  30.9 0.3 multiply_convert_fusion
  31.3 0.0 copy-done.1
  31.3 0.3 convolution_convert_fusion
  31.6 0.0 copy-done.2
  31.7 1.1 fusion.14
  32.8 0.0 copy-done.3
  32.8 0.3 convolution_convert_fusion.1
  33.2 7.0 %fusion.74 = (f32[4,8,256]{2,1,0:T(8,128)S(1)}, f32[4,8,256,256]{2,3,1,0:T(8,128)}) fusion(f32[256]{0:T(256)S(1)} %get-tuple-element.43, bf16[256,4,8,32]{0,3,2,1:T(8,128)(2,1)} %bitcast.120, bf16[256,4,8,32]{0,3,2,1:T(8,128)(2,1)S(1)} %bitcast.119), kind=kOutput, calls=%fused_computation.100 | convolution fusion | flops 140509440 | bytes 9470976 | tf_op jit(solution)/shard_map/sub | solution.py:55
  40.2 5.3 %fusion.5 = f32[4,8,32,256]{3,2,1,0:T(8,128)} fusion(bf16[256,4,8,32]{0,3,2,1:T(8,128)(2,1)S(1)} %bitcast.118, f32[4,8,256,256]{2,3,1,0:T(8,128)} %get-tuple-element.47, f32[4,8,256]{2,1,0:T(8,128)S(1)} %get-tuple-element.46), kind=kOutput, calls=%fused_computation.8 | convolution fusion | flops 138412032 | bytes 9994240 | tf_op jit(solution)/shard_map/khst,tkhd->skhd/dot_general | solution.py:57
  45.5 1.6 %copy.159 = f32[256,4,256]{2,0,1:T(8,128)S(1)} copy(f32[256,4,256]{0,2,1:T(8,128)} %bitcast.116) | data formatting | bytes 2097152 | tf_op jit(solution)/shard_map/reshape | solution.py:58
  47.1 0.0 copy-done.6
  47.1 1.4 %convert_reduce_fusion = (f32[256,4]{0,1:T(4,128)S(1)}, bf16[256,4,256]{0,2,1:T(8,128)(2,1)}) fusion(f32[256,4,256]{0,2,1:T(8,128)S(1)} %copy.161, bf16[256,256]{1,0:T(8,128)(2,1)S(1)} %copy-done.6, f32[256,4,256]{2,0,1:T(8,128)S(1)} %copy.159, bf16[256,4,256]{2,0,1:T(8,128)(2,1)S(1)} %multiply_convert_fusion, bf16[256,256]{1,0:T(8,128)(2,1)S(1)} %copy-done.7), kind=kOutput, calls=%fused_computation.12 | convolution fusion | flops 270793728 | bytes 3411968 | tf_op jit(solution)/shard_map/dot_general | solution.py:61
  48.5 1.2 fusion.29
  49.8 2.7 %convert_reduce_fusion.1 = (f32[256,4]{0,1:T(4,128)S(1)}, bf16[256,4,256]{0,2,1:T(8,128)(2,1)S(1)}) fusion(bf16[1024,256]{1,0:T(8,128)(2,1)S(1)} %copy-done, bf16[256,4,256]{0,2,1:T(8,128)(2,1)} %get-tuple-element.49, bf16[256,1024]{1,0:T(8,128)(2,1)} %param.26, f32[256,4]{0,1:T(4,128)S(1)} %add_rsqrt_fusion.2, f32[256,4]{0,1:T(4,128)S(1)} %broadcast_multiply_fusion.2), kind=kOutput, calls=%fused_computation.22 | convolution fusion | flops 1078197248 | bytes 2109440 | tf_op jit(solution)/shard_map/dot_general | solution.py:69
  52.4 0.0 copy-start.4
  52.5 0.2 fusion.31
  52.6 0.9 fusion.27
  53.5 0.0 all-gather.2.cloned.1.call-update
  53.5 0.0 copy-done.12
  53.6 0.3 fusion.28
  53.8 0.2 copy.169
  54.0 0.3 reshape.153
  54.3 8.9 %all_to_all.63 = bf16[16,2,1024]{2,1,0:T(2,128)(2,1)S(1)} all-to-all(bf16[16,2,1024]{2,1,0:T(2,128)(2,1)S(1)} %reshape.153), channel_id=1, replica_groups=mesh['seq'=16,'res'=2] {'seq'}, dimensions={0} | all-to-all | bytes 131072 | tf_op jit(solution)/shard_map/all_to_all | solution.py:164
  63.2 0.2 reshape.154
  63.5 8.2 %all_gather.7 = bf16[16,128,32]{2,0,1:T(8,128)(2,1)S(1)} all-gather(bf16[16,64,32]{2,0,1:T(8,128)(2,1)S(1)} %bitcast.115), channel_id=1, replica_groups=mesh['seq'=16,'res'=2] {'res'}, dimensions={1}, use_global_device_ids=true | all-gather | bytes 196608 | tf_op jit(solution)/shard_map/all_gather | solution.py:167
  71.7 1.2 reshape.155
  72.9 6.3 %all-to-all-start.3 = ((bf16[16,2,2048]{2,1,0:T(2,128)(2,1)}), bf16[16,2,2048]{2,1,0:T(2,128)(2,1)S(1)}, u32[]{:S(2)}, u32[]{:S(2)}) async-start(bf16[16,2,2048]{2,1,0:T(2,128)(2,1)} %reshape.155), calls=%async_computation.3 | async-start | bytes 262144 | tf_op jit(solution)/shard_map/all_to_all | solution.py:168
  79.2 1.1 copy.164
  80.2 6.2 %all-to-all-done.3 = bf16[16,2,2048]{2,1,0:T(2,128)(2,1)S(1)} async-done(((bf16[16,2,2048]{2,1,0:T(2,128)(2,1)}), bf16[16,2,2048]{2,1,0:T(2,128)(2,1)S(1)}, u32[]{:S(2)}, u32[]{:S(2)}) %all-to-all-start.3) | async-done | bytes 131104 | tf_op jit(solution)/shard_map/all_to_all | solution.py:168
  86.5 5.3 %all-to-all-start.1 = ((bf16[256,4,256]{2,1,0:T(4,128)(2,1)}), bf16[256,4,256]{2,1,0:T(4,128)(2,1)S(1)}, u32[]{:S(2)}, u32[]{:S(2)}) async-start(bf16[256,4,256]{2,1,0:T(4,128)(2,1)} %copy.164), calls=%async_computation.1 | async-start | bytes 1048576 | tf_op jit(solution)/shard_map/all_to_all | solution.py:163
  91.8 0.0 copy-done.4
  91.8 0.1 dynamic-slice_convert_fusion
  91.9 0.7 convert_multiply_fusion
  92.6 0.1 dynamic-slice_convert_fusion.1
  92.6 0.1 multiply_maximum_fusion
  92.7 0.3 reshape.156
  93.0 0.1 copy.173
  93.1 0.1 bitcast_multiply_fusion
  93.3 0.3 copy.174
  93.6 11.8 %all-to-all-done.1 = bf16[256,4,256]{2,1,0:T(4,128)(2,1)S(1)} async-done(((bf16[256,4,256]{2,1,0:T(4,128)(2,1)}), bf16[256,4,256]{2,1,0:T(4,128)(2,1)S(1)}, u32[]{:S(2)}, u32[]{:S(2)}) %all-to-all-start.1) | async-done | bytes 524320 | tf_op jit(solution)/shard_map/all_to_all | solution.py:163
  105.4 0.1 copy.165
  105.5 1.0 copy.177
  106.5 4.4 %convert_bitcast_fusion = bf16[8,64,32,32]{2,3,0,1:T(8,128)(2,1)} fusion(bf16[256,64,32]{0,2,1:T(8,128)(2,1)} %all-gather.2.cloned.1.call-done, bf16[64]{0:T(256)(128)(2,1)S(1)} %get-tuple-element.45, bf16[256,8,32]{0,2,1:T(8,128)(2,1)S(1)} %copy.174), kind=kOutput, calls=%fused_computation.5 | convolution fusion | flops 271056896 | bytes 2228352 | tf_op jit(solution)/shard_map/while/body/eval_jaxpr/sic,sje->ijce/dot_general | solution.py:92
  110.9 0.0 copy-start.10
  110.9 7.7 %copy.175 = bf16[8,64,32,32]{1,3,2,0:T(8,128)(2,1)S(1)} copy(bf16[8,64,32,32]{2,3,0,1:T(8,128)(2,1)} %convert_bitcast_fusion) | data formatting | bytes 2097152 | tf_op jit(solution)/shard_map/while/body/eval_jaxpr/convert_element_type | solution.py:94
  118.7 0.8 fusion.81
  119.5 0.3 multiply_reduce_fusion.1
  119.8 1.2 fusion.26
  (30 shorter events, 0.2 us)
Async XLA Ops:
  7.2 42.6 %copy-start = (bf16[1024,256]{1,0:T(8,128)(2,1)S(1)}, bf16[1024,256]{1,0:T(8,128)(2,1)}, u32[]{:S(2)}) copy-start(bf16[1024,256]{1,0:T(8,128)(2,1)} %param.27) | copy-start | bytes 1572868
  9.4 20.1 %all-to-all-start = ((bf16[16,16,4,256]{3,0,2,1:T(8,128)(2,1)}), bf16[16,16,4,256]{3,0,2,1:T(8,128)(2,1)S(1)}, u32[]{:S(2)}, u32[]{:S(2)}) async-start(bf16[16,16,4,256]{3,0,2,1:T(8,128)(2,1)} %bitcast), calls=%async_computation | async-start | bytes 1048576 | tf_op jit(solution)/shard_map/all_to_all | solution.py:152
  15.9 90.6 %all-gather.2.cloned.1.call-start = ((), (), s32[]{:S(2)}) async-start(), calls=%async_computation.4 | async-start | bytes 1114112 | tf_op jit(solution)/shard_map/all_gather | solution.py:166
  29.7 1.6 %copy-start.1 = (bf16[256,256]{1,0:T(8,128)(2,1)S(1)}, bf16[256,256]{1,0:T(8,128)(2,1)}, u32[]{:S(2)}) copy-start(bf16[256,256]{1,0:T(8,128)(2,1)} %param.22) | copy-start | bytes 393220
  30.4 1.3 %copy-start.2 = (bf16[256,256]{1,0:T(8,128)(2,1)S(1)}, bf16[256,256]{1,0:T(8,128)(2,1)}, u32[]{:S(2)}) copy-start(bf16[256,256]{1,0:T(8,128)(2,1)} %param.21) | copy-start | bytes 393220
  30.5 2.3 %copy-start.3 = (bf16[256,256]{1,0:T(8,128)(2,1)S(1)}, bf16[256,256]{1,0:T(8,128)(2,1)}, u32[]{:S(2)}) copy-start(bf16[256,256]{1,0:T(8,128)(2,1)} %param.23) | copy-start | bytes 393220
  40.2 6.9 %copy-start.6 = (bf16[256,256]{1,0:T(8,128)(2,1)S(1)}, bf16[256,256]{1,0:T(8,128)(2,1)}, u32[]{:S(2)}) copy-start(bf16[256,256]{1,0:T(8,128)(2,1)} %param.25) | copy-start | bytes 393220
  40.2 6.9 %copy-start.7 = (bf16[256,256]{1,0:T(8,128)(2,1)S(1)}, bf16[256,256]{1,0:T(8,128)(2,1)}, u32[]{:S(2)}) copy-start(bf16[256,256]{1,0:T(8,128)(2,1)} %param.24) | copy-start | bytes 393220
  48.5 4.1 %copy-start.11 = (bf16[256,32]{0,1:T(8,128)(2,1)S(1)}, bf16[256,32]{0,1:T(8,128)(2,1)}, u32[]{:S(2)}) copy-start(bf16[256,32]{0,1:T(8,128)(2,1)} %param.29) | copy-start | bytes 49156
  48.5 5.0 %copy-start.12 = (bf16[256,32]{0,1:T(8,128)(2,1)S(1)}, bf16[256,32]{0,1:T(8,128)(2,1)}, u32[]{:S(2)}) copy-start(bf16[256,32]{0,1:T(8,128)(2,1)} %param.28) | copy-start | bytes 49156
  52.4 39.3 %copy-start.4 = (s32[128]{0:T(128)S(1)}, s32[128]{0:T(128)}, u32[]{:S(2)}) copy-start(s32[128]{0:T(128)} %param.20) | copy-start | bytes 1540
  72.9 13.6 %all-to-all-start.3 = ((bf16[16,2,2048]{2,1,0:T(2,128)(2,1)}), bf16[16,2,2048]{2,1,0:T(2,128)(2,1)S(1)}, u32[]{:S(2)}, u32[]{:S(2)}) async-start(bf16[16,2,2048]{2,1,0:T(2,128)(2,1)} %reshape.155), calls=%async_computation.3 | async-start | bytes 262144 | tf_op jit(solution)/shard_map/all_to_all | solution.py:168
  86.5 18.9 %all-to-all-start.1 = ((bf16[256,4,256]{2,1,0:T(4,128)(2,1)}), bf16[256,4,256]{2,1,0:T(4,128)(2,1)S(1)}, u32[]{:S(2)}, u32[]{:S(2)}) async-start(bf16[256,4,256]{2,1,0:T(4,128)(2,1)} %copy.164), calls=%async_computation.1 | async-start | bytes 1048576 | tf_op jit(solution)/shard_map/all_to_all | solution.py:163
  110.9 7.7 %copy-start.5 = (bf16[1024,128]{1,0:T(8,128)(2,1)S(1)}, bf16[1024,128]{1,0:T(8,128)(2,1)}, u32[]{:S(2)}) copy-start(bf16[1024,128]{1,0:T(8,128)(2,1)} %param.30) | copy-start | bytes 786436
  110.9 7.7 %copy-start.8 = (bf16[8,64,128]{2,1,0:T(8,128)(2,1)S(1)}, bf16[8,64,128]{2,1,0:T(8,128)(2,1)}, u32[]{:S(2)}) copy-start(bf16[8,64,128]{2,1,0:T(8,128)(2,1)} %param.18) | copy-start | bytes 393220
  110.9 7.7 %copy-start.13 = (f32[128]{0:T(128)S(1)}, f32[128]{0:T(128)}, u32[]{:S(2)}) copy-start(f32[128]{0:T(128)} %param.31) | copy-start | bytes 1540
  110.9 8.9 %copy-start.9 = (bf16[512,128]{1,0:T(8,128)(2,1)S(1)}, bf16[512,128]{1,0:T(8,128)(2,1)}, u32[]{:S(2)}) copy-start(bf16[512,128]{1,0:T(8,128)(2,1)} %param.33) | copy-start | bytes 393220
  110.9 8.9 %copy-start.10 = (bf16[128,512]{1,0:T(8,128)(2,1)S(1)}, bf16[128,512]{1,0:T(8,128)(2,1)}, u32[]{:S(2)}) copy-start(bf16[128,512]{1,0:T(8,128)(2,1)} %param.32) | copy-start | bytes 393220
Sparse Core Ops, SparseCore 0:
  53.7 37.6 all-gather.1
where the time goes:
time: 130 us; the launch traced here: 128 us
  waiting for transfers between devices  29.5 us (23%)
  matrix products  25.8 us (20%)
  starting transfers between devices  18.2 us (14%)
  blocking collectives  17.2 us (13%)
  local copies, waits for them, and re-layouts  16.8 us (13%)
  between operations  14.4 us (11%)
  other arithmetic  5.9 us (5%)
    all_to_all x1, waiting for transfers between devices, per_device(): lax.all_to_all(alignment_columns, 'seq', split_axis=0, concat_axis=1, til...  11.8 us
    all_to_all x1, waiting for transfers between devices, per_device(): lax.all_to_all(grouped, 'seq', split_axis=1, concat_axis=0, tiled=True)  11.5 us
    all_to_all x1, blocking collectives, per_device(): lax.all_to_all(left_column_set, 'seq', split_axis=0, concat_axis=1, tiled...  8.94 us
    all_gather x1, blocking collectives, per_device(): left_wide = lax.all_gather(left_home, 'res', axis=1, tiled=True)  8.23 us
    convert_element_type x1, local copies, waits for them, and re-layouts, pair_block_update(): outer = jnp.einsum('sic,sje->ijce', left_rows, right_full, preferred_elem...  7.69 us
    sub x1, matrix products, column_delta(): exponent = jnp.exp(scores - peak_score)  7.03 us
    all_to_all x1, starting transfers between devices, per_device(): lax.all_to_all(grouped, 'seq', split_axis=1, concat_axis=0, tiled=True)  6.52 us
    all_to_all x1, starting transfers between devices, per_device(): lax.all_to_all(left_wide, 'seq', split_axis=1, concat_axis=0, tiled=True)  6.28 us
  transfers between devices with their start and end apart: 4, of which 3 were waited for; matrix products, arithmetic and copies ran while one was open for 6% of the time, Pallas kernels for 0%

commit v1 on v0

v1 whole, which is shorter than its diff:
```python
import functools
import math

import jax
import jax.numpy as jnp
from jax import lax
from jax.experimental import pallas as pl
from jax.experimental.pallas import tpu as pltpu
from jax.sharding import PartitionSpec as P

FOCUS_NUMBER = 8
FOCUS_BREADTH = 32
COUPLING_DIM = 32
OWNED = 4
PACK = 4

epsilon = 1e-05
mask_fill = 1000000000.0
F32 = jnp.float32
BF16 = jnp.bfloat16


def layer_norm(values):
    centre = values - jnp.mean(values, axis=-1, keepdims=True)
    spread = jnp.mean(centre * centre, axis=-1, keepdims=True)
    return centre * lax.rsqrt(spread + epsilon)


def mm(a, b):
    return jnp.dot(a, b, preferred_element_type=F32)


def mm_nt(a, b):
    return lax.dot_general(a, b, (((1,), (1,)), ((), ())), preferred_element_type=F32)


def kernel(
    n,
    res_n,
    x_ref,
    pair_ref,
    rowm_ref,
    keep_ref,
    wq,
    wk,
    wv,
    wg,
    wm,
    wu,
    wn,
    w1,
    w2,
    wo,
    bias_ref,
    wpu,
    wpd,
    msa_out,
    pair_out,
    proj_w,
    wm_v,
    wu_v,
    wn_v,
    w1_v,
    w2_v,
    wo_v,
    wpu_v,
    wpd_v,
    xcol,
    ycol,
    n3,
    lsend,
    lbuf,
    lexp,
    rbuf,
    keepj,
    w_sem,
    own_sem,
    in_send,
    in_recv,
    l_send,
    l_recv,
    r_send,
    rz_recv,
    ry_recv,
    rc_recv,
    o_send,
    o_recv,
):
    me = lax.axis_index("seq")
    my_res = lax.axis_index("res")
    cols, shard_rows, width = x_ref.shape
    rows = n * shard_rows
    lines = n // 4
    row_span = pair_ref.shape[0]

    def remote(src, dst, send, recv, where):
        return pltpu.make_async_remote_copy(
            src_ref=src,
            dst_ref=dst,
            send_sem=send,
            recv_sem=recv,
            device_id=where,
            device_id_type=pl.DeviceIdType.MESH,
        )

    def at(s):
        return (s, my_res)

    def drain(ref, sem):
        pltpu.make_async_copy(ref, ref, sem).wait()

    my_rows = pl.ds(pl.multiple_of(me * shard_rows, shard_rows), shard_rows)
    for c in range(OWNED):

        @pl.loop(1, n)
        def _(k, c=c):
            dst = lax.rem(me + k, n)
            remote(
                x_ref.at[dst * OWNED + c],
                xcol.at[c, my_rows],
                in_send.at[c],
                in_recv.at[c],
                at(dst),
            ).start()

    own = pltpu.make_async_copy(
        x_ref.at[pl.ds(me * OWNED, OWNED)], xcol.at[:, my_rows], own_sem
    )
    own.start()
    fetches = [
        (wq, proj_w.at[:, 0:width]),
        (wk, proj_w.at[:, width : 2 * width]),
        (wv, proj_w.at[:, 2 * width : 3 * width]),
        (wg, proj_w.at[:, 3 * width : 4 * width]),
        (wm, wm_v),
        (wu, wu_v),
        (wn, wn_v),
        (w1, w1_v),
        (w2, w2_v),
        (wo, wo_v),
        (wpu, wpu_v),
        (wpd, wpd_v),
    ]
    fetches = [pltpu.make_async_copy(s, d, w_sem.at[i]) for i, (s, d) in enumerate(fetches)]
    for f in fetches:
        f.start()

    sub = lax.broadcasted_iota(jnp.int32, (8, 128), 0)
    for d in range(n):
        flags = [
            keep_ref[my_res * cols + d * OWNED + m].astype(F32) for m in range(OWNED)
        ]
        tile = jnp.full((8, 128), flags[0], F32)
        for m in range(1, OWNED):
            tile = jnp.where(lax.rem(sub, OWNED) == m, flags[m], tile)
        keepj[d] = tile

    row_flags = rowm_ref[...].astype(F32)
    bias = (row_flags - 1.0) * mask_fill
    lane = lax.broadcasted_iota(jnp.int32, (1, width), 1)
    head_masks = [
        (lane // FOCUS_BREADTH == h).astype(F32).astype(BF16) for h in range(FOCUS_NUMBER)
    ]
    scaling = 1.0 / math.sqrt(FOCUS_BREADTH)
    own.wait()
    for f in fetches:
        f.wait()

    def column(c, carry):
        drain(xcol.at[c, pl.ds(0, (n - 1) * shard_rows)], in_recv.at[c])
        inputs = xcol[c].astype(F32)
        normed = layer_norm(inputs).astype(BF16)
        q = (mm(normed, proj_w[:, 0:width]) * scaling).astype(BF16)
        k = mm(normed, proj_w[:, width : 2 * width]).astype(BF16)
        v = mm(normed, proj_w[:, 2 * width : 3 * width]).astype(BF16)
        top = jnp.zeros((rows, width), F32)
        low = jnp.zeros((rows, width), F32)
        for h in range(FOCUS_NUMBER):
            scores = mm_nt(q * head_masks[h], k) + bias
            peak = jnp.max(scores, axis=-1, keepdims=True)
            e = jnp.exp(scores - peak).astype(BF16)
            top = top + mm(e, v * head_masks[h])
            low = low + mm(e, jnp.broadcast_to(head_masks[h], (rows, width)))
        gate = jax.nn.sigmoid(mm(normed, proj_w[:, 3 * width : 4 * width]))
        gated = (gate * (top / low)).astype(BF16)
        after = (inputs + mm(gated, wm_v[...])).astype(BF16)
        normed_two = layer_norm(after.astype(F32)).astype(BF16)
        hidden = jnp.maximum(mm(normed_two, wu_v[...]), 0.0).astype(BF16)
        updated = (after.astype(F32) + mm(hidden, wn_v[...])).astype(BF16)
        ycol[c] = updated
        n3[c] = layer_norm(updated.astype(F32)).astype(BF16)
        return carry

    lax.fori_loop(0, OWNED, column, 0)

    lanes = lax.broadcasted_iota(jnp.int32, (1, 128), 1)
    tall = lax.broadcasted_iota(jnp.int32, (128, width), 0)
    left = jnp.zeros((rows, 128), F32)
    right = jnp.zeros((128, rows), F32)
    for c in range(OWNED):
        here = (lanes // COUPLING_DIM == c).astype(F32).astype(BF16)
        left = left + mm(n3[c], w1_v[...] * here)
        there = (lax.rem(tall, OWNED) == c).astype(F32).astype(BF16)
        right = right + mm_nt(w2_v[...] * there, n3[c])
    right = (right * row_flags).astype(BF16)
    my_block = pl.ds(pl.multiple_of(me * 32, 32), 32)
    for k in range(PACK):
        rbuf[k, my_block, :] = right[k * 32 : (k + 1) * 32]
    lsend[...] = left.astype(BF16)

    line = me // 4
    spot = lax.rem(me, 4)
    core = lax.rem(me, 2)
    y_pair = line * 4 + lax.rem(spot + 2, 4)
    c_pair = me + 1 - 2 * core

    def pass_on(block, sem, to):
        part = rbuf.at[:, pl.ds(pl.multiple_of(block * 32, 32), 32)]
        remote(part, part, r_send, sem, at(to)).start()

    def got(block, sem):
        drain(rbuf.at[:, pl.ds(pl.multiple_of(block * 32, 32), 32)], sem)

    def line_block(k):
        z = lax.rem(line + lines - k, lines)
        return z, z * 4 + spot, z * 4 + lax.rem(spot + 2, 4)

    for k in range(1, lines):
        pass_on(me, rz_recv.at[line], lax.rem(line + k, lines) * 4 + spot)
    pass_on(me, ry_recv.at[line], y_pair)
    pass_on(me, rc_recv.at[0, line], c_pair)

    q_row = my_res * (n // res_n) + me // res_n
    slot = lax.rem(me, res_n)
    for r in range(res_n):
        local = jnp.logical_and(q_row == me, my_res == r)

        @pl.when(local)
        def _():
            pltpu.make_async_copy(lsend, lbuf.at[slot], l_recv.at[slot]).start()

        @pl.when(jnp.logical_not(local))
        def _(r=r):
            remote(lsend, lbuf.at[slot], l_send.at[r], l_recv.at[slot], (q_row, r)).start()

    for k in range(1, lines):
        z, block, _ = line_block(k)
        got(block, rz_recv.at[z])
        pass_on(block, ry_recv.at[z], y_pair)
        pass_on(block, rc_recv.at[0, z], c_pair)
    for k in range(lines):
        z, _, block = line_block(k)
        got(block, ry_recv.at[z])
        pass_on(block, rc_recv.at[1, z], c_pair)

    @pl.loop(1, n)
    def _(k):
        dst = lax.rem(me + k, n)
        remote(
            ycol.at[:, pl.ds(pl.multiple_of(dst * shard_rows, shard_rows), shard_rows)],
            msa_out.at[pl.ds(me * OWNED, OWNED)],
            o_send,
            o_recv,
            at(dst),
        ).start()

    home = pltpu.make_async_copy(
        ycol.at[:, my_rows], msa_out.at[pl.ds(me * OWNED, OWNED)], own_sem
    )
    home.start()

    for t in range(res_n):
        drain(lbuf.at[t], l_recv.at[t])
        block = lbuf[t].astype(F32)
        turned = [block] + [pltpu.roll(block, 32 * a, 1) for a in range(1, PACK)]
        for k in range(PACK):
            inside = lanes // COUPLING_DIM == k
            for m in range(OWNED):
                tile = jnp.where(inside, turned[(k - m) % PACK], 0.0).astype(BF16)
                i = t * OWNED + m
                lexp[k, :, i * 128 : (i + 1) * 128] = tile
    for k in range(lines):
        z, block, other = line_block(k)
        got(z * 4 + lax.rem(spot, 4) + 1 - 2 * core, rc_recv.at[0, z])
        got(z * 4 + lax.rem(spot + 2, 4) + 1 - 2 * core, rc_recv.at[1, z])

    live = jnp.sum(row_flags, axis=-1, keepdims=True)
    sub3 = lax.broadcasted_iota(jnp.int32, (1, 8, 128), 1)
    first = sub3 < 4
    flags_j = keepj[...]
    add_bias = bias_ref[...].reshape(1, 1, 128)
    half = n // 2

    def pair_rows(a, b):
        return jnp.where(first, a, pltpu.roll(b, 4, 1)), jnp.where(first, pltpu.roll(a, 4, 1), b)

    for ip in range(row_span // 2):
        outer = jnp.zeros((n * 32, 256), F32)
        for k in range(PACK):
            outer = outer + mm(rbuf[k], lexp[k, :, ip * 256 : (ip + 1) * 256])
        outer = outer.reshape(n, 4, 8, 256)
        sums = []
        for p in range(2):
            total = jnp.zeros((n * 8, 256), F32)
            for g in range(4):
                piece = outer[:, g, :, p * 128 : (p + 1) * 128].reshape(n * 8, 128).astype(BF16)
                total = total + mm(piece, wo_v[g * 128 : (g + 1) * 128, :])
            total = total.reshape(n, 8, 256)
            total = jnp.where(first, total[:, :, :128], total[:, :, 128:])
            sums.append(total + pltpu.roll(total, 4, 1))
        total = jnp.where(first, sums[0], sums[1])
        i = 2 * ip
        keep_a = keep_ref[me * row_span + i].astype(F32)
        keep_b = keep_ref[me * row_span + i + 1].astype(F32)
        flags = jnp.where(first, keep_a, keep_b) * flags_j
        norm = live.reshape(1, 1, 1) * flags
        mean = (total * flags + add_bias) / jnp.maximum(norm, 1.0)
        a = pair_ref[i].astype(F32).reshape(half, 8, 128)
        b = pair_ref[i + 1].astype(F32).reshape(half, 8, 128)
        a, b = pair_rows(a, b)
        old = jnp.stack([a, b], axis=1).reshape(n, 8, 128)
        mid = (old + mean).reshape(n * 8, 128).astype(BF16)
        normed = layer_norm(mid.astype(F32)).astype(BF16)
        hidden = jnp.maximum(mm(normed, wpu_v[...]), 0.0).astype(BF16)
        new = mid.astype(F32) + mm(hidden, wpd_v[...])
        new = new.reshape(half, 2, 8, 128)
        a, b = pair_rows(new[:, 0], new[:, 1])
        pair_out[i] = a.reshape(cols, 128).astype(BF16)
        pair_out[i + 1] = b.reshape(cols, 128).astype(BF16)

    home.wait()
    drain(msa_out.at[pl.ds(0, (n - 1) * OWNED)], o_recv)
    for c in range(OWNED):
        drain(xcol.at[c, pl.ds(0, (n - 1) * shard_rows)], in_send.at[c])
    drain(ycol.at[:, pl.ds(0, (n - 1) * shard_rows)], o_send)
    drain(rbuf.at[:, pl.ds(0, (4 * lines - 1) * 32)], r_send)
    for r in range(res_n):

        @pl.when(jnp.logical_not(jnp.logical_and(q_row == me, my_res == r)))
        def _(r=r):
            drain(lsend, l_send.at[r])


def per_device(
    homolog_embedding,
    pair_features,
    row_present_mask,
    residue_keep_mask,
    query_weight,
    key_weight,
    content_matrix,
    sigmoid_switch_matrix,
    focus_merge_matrix,
    widening_matrix,
    narrowing_matrix,
    first_factor_matrix,
    second_factor_matrix,
    outer_product_weight,
    outer_product_bias,
    pair_up_weight,
    pair_down_weight,
):
    n = lax.axis_size("seq")
    res_n = lax.axis_size("res")
    shard_rows, cols, width = homolog_embedding.shape
    row_span, _, c_z = pair_features.shape
    rows = shard_rows * n
    assert cols == OWNED * n and n % 4 == 0 and n % res_n == 0
    hidden = widening_matrix.shape[1]
    x = homolog_embedding.transpose(1, 0, 2)
    w1 = jnp.tile(first_factor_matrix, (1, OWNED))
    w2 = second_factor_matrix.T.reshape(COUPLING_DIM // PACK, PACK, 1, width)
    w2 = jnp.broadcast_to(
        w2.transpose(1, 0, 2, 3), (PACK, COUPLING_DIM // PACK, OWNED, width)
    ).reshape(128, width)
    wo = outer_product_weight.reshape(COUPLING_DIM, 4, 2, PACK, c_z)
    wo = wo.transpose(1, 3, 0, 2, 4).reshape(4 * PACK * COUPLING_DIM, 2 * c_z)
    vmem = pl.BlockSpec(memory_space=pltpu.VMEM)
    smem = pl.BlockSpec(memory_space=pltpu.SMEM)
    anyw = pl.BlockSpec(memory_space=pl.ANY)
    dma = pltpu.SemaphoreType.DMA
    lines = n // 4
    msa, pair = pl.pallas_call(
        functools.partial(kernel, n, res_n),
        out_shape=(
            jax.ShapeDtypeStruct((cols, shard_rows, width), BF16),
            jax.ShapeDtypeStruct(pair_features.shape, BF16),
        ),
        in_specs=[vmem, vmem, vmem, smem] + [anyw] * 10 + [vmem] + [anyw] * 2,
        out_specs=(vmem, vmem),
        scratch_shapes=[
            pltpu.VMEM((width, 4 * width), BF16),
            pltpu.VMEM(focus_merge_matrix.shape, BF16),
            pltpu.VMEM(widening_matrix.shape, BF16),
            pltpu.VMEM(narrowing_matrix.shape, BF16),
            pltpu.VMEM(w1.shape, BF16),
            pltpu.VMEM(w2.shape, BF16),
            pltpu.VMEM(wo.shape, BF16),
            pltpu.VMEM(pair_up_weight.shape, BF16),
            pltpu.VMEM(pair_down_weight.shape, BF16),
            pltpu.VMEM((OWNED, rows, width), BF16),
            pltpu.VMEM((OWNED, rows, width), BF16),
            pltpu.VMEM((OWNED, rows, width), BF16),
            pltpu.VMEM((rows, 128), BF16),
            pltpu.VMEM((res_n, rows, 128), BF16),
            pltpu.VMEM((PACK, rows, row_span * 128), BF16),
            pltpu.VMEM((PACK, n * 32, rows), BF16),
            pltpu.VMEM((n, 8, 128), F32),
            dma((12,)),
            dma,
            dma((OWNED,)),
            dma((OWNED,)),
            dma((res_n,)),
            dma((res_n,)),
            dma,
            dma((lines,)),
            dma((lines,)),
            dma((2, lines)),
            dma,
            dma,
        ],
        compiler_params=pltpu.CompilerParams(
            has_side_effects=True, vmem_limit_bytes=60 * 1024 * 1024
        ),
    )(
        x,
        pair_features,
        row_present_mask.reshape(1, rows),
        residue_keep_mask,
        query_weight,
        key_weight,
        content_matrix,
        sigmoid_switch_matrix,
        focus_merge_matrix,
        widening_matrix,
        narrowing_matrix,
        w1,
        w2,
        wo,
        outer_product_bias.reshape(1, c_z),
        pair_up_weight,
        pair_down_weight,
    )
    return (msa.transpose(1, 0, 2), pair)


def solution(mesh):
    placed = (P("seq", "res", None), P("seq", "res", None)) + (P(),) * 15
    return jax.shard_map(
        per_device,
        mesh=mesh,
        in_specs=placed,
        out_specs=(P("seq", "res", None), P("seq", "res", None)),
        check_vma=False,
    )
```

time: 130 us -> 69 us (0.53); the launches traced: 128 us -> 68.6 us
  Pallas kernels: 0 us -> 60.9 us
  waiting for transfers between devices: 29.5 us -> 0 us
  matrix products: 25.8 us -> 0 us
  starting transfers between devices: 18.2 us -> 0 us
  blocking collectives: 17.2 us -> 0 us
  between operations: 14.4 us -> 0.68 us
  local copies, waits for them, and re-layouts: 16.8 us -> 7.06 us
  other arithmetic: 5.9 us -> 0 us
    pallas_call x0 -> x1, Pallas kernels: none -> 60.9 us  [per_device(): pl.pallas_call(functools.partial(kernel, n, res_n), out_shape=(jax.ShapeD...]
    all_to_all x3 -> x0, waiting for transfers between devices: 29.5 us -> none  [the longest x1 11.8 us: per_device(): lax.all_to_all(alignment_columns, 'seq', split_axis=0, concat_axis=1, til...]
    dot_general x11 -> x0, matrix products: 18.8 us -> none  [the longest x1 5.34 us: column_delta(): jnp.einsum('khst,tkhd->skhd', probs, values_all, preferred_element_type=j...]
    all_to_all x3 -> x0, starting transfers between devices: 18.1 us -> none  [the longest x1 6.52 us: per_device(): lax.all_to_all(grouped, 'seq', split_axis=1, concat_axis=0, tiled=True)]
    convert_element_type x5 -> x0, local copies, waits for them, and re-layouts: 9.34 us -> none  [the longest x1 7.69 us: pair_block_update(): outer = jnp.einsum('sic,sje->ijce', left_rows, right_full, preferred_elem...]
    all_to_all x1 -> x0, blocking collectives: 8.94 us -> none  [per_device(): lax.all_to_all(left_column_set, 'seq', split_axis=0, concat_axis=1, tiled...]
    all_gather x1 -> x0, blocking collectives: 8.23 us -> none  [per_device(): left_wide = lax.all_gather(left_home, 'res', axis=1, tiled=True)]
    sub x1 -> x0, matrix products: 7.03 us -> none  [column_delta(): exponent = jnp.exp(scores - peak_score)]
  transfers between devices with their start and end apart: 4 -> 0, of which waited for: 3 -> 0; matrix products, arithmetic and copies ran while one was open for 6% -> 0% of each run, Pallas kernels for 0% -> 0%
where the time goes in v1:
time: 69 us; the launch traced here: 68.6 us
  Pallas kernels  60.9 us (88%)
  local copies, waits for them, and re-layouts  7.06 us (10%)
    pallas_call x1, Pallas kernels, per_device(): pl.pallas_call(functools.partial(kernel, n, res_n), out_shape=(jax.ShapeD...  60.9 us
    unnamed x12, local copies, waits for them, and re-layouts  4.65 us

profile of v1, /device:TPU:15, one launch (start us, length us, event | category | flops | bytes accessed | tf_op | source)
XLA Modules:
  0.0 68.6 jit_solution(13963530058495299771)
XLA Ops:
  0.6 0.0 copy-start.1
  0.6 0.8 %reshape.27 = bf16[8,4,1,256]{3,1,0,2:T(4,128)(2,1)S(1)} reshape(bf16[32,256]{1,0:T(8,128)(2,1)} %bitcast.25) | data formatting | bytes 32768 | tf_op jit(solution)/shard_map/reshape | solution.py:372
  1.4 0.0 copy-start.3
  1.5 0.7 reshape.28.w2
  2.1 0.1 copy-done.3
  2.2 0.7 %copy.27.w1 = bf16[256,128]{1,0:T(8,128)(2,1)} copy(bf16[256,128]{0,1:T(8,128)(2,1)S(1)} %bitcast.22) | data formatting | bytes 131072 | tf_op jit(solution)/shard_map/tile | solution.py:371
  2.9 0.0 copy-done.1
  2.9 0.0 copy-start
  2.9 0.2 copy.26
  3.1 0.7 %copy.33 = bf16[64,8,2,128]{3,1,2,0:T(8,128)(2,1)} copy(bf16[64,8,2,128]{3,2,1,0:T(2,128)(2,1)S(1)} %bitcast.20) | data formatting | bytes 524288
  3.9 0.1 copy-done
  4.0 1.1 %copy.32 = bf16[16,64,256]{2,0,1:T(8,128)(2,1)} copy(bf16[16,64,256]{2,1,0:T(8,128)(2,1)S(1)} %copy-done) | data formatting | bytes 1048576 | tf_op args[0]
  5.0 60.9 %shard_map.176 = (bf16[64,16,256]{2,1,0:T(8,128)(2,1)}, bf16[8,64,128]{2,1,0:T(8,128)(2,1)}) custom-call(bf16[64,16,256]{2,1,0:T(8,128)(2,1)} %bitcast.18, bf16[8,64,128]{2,1,0:T(8,128)(2,1)} %pair_ref.1, s32[1,256]{1,0:T(1,128)} %bitcast.26, s32[128]{0:T(128)} %keep_ref.1, bf16[256,256]{1,0:T(8,128)(2,1)} %wq.1, bf16[256,256]{1,0:T(8,128)(2,1)} %wk.1, ...), custom_call_target="tpu_custom_call" | custom-call | tf_op jit(solution)/shard_map/pallas_call | solution.py:383
  65.9 0.0 copy-start.2
  66.0 2.0 %copy.28 = bf16[16,64,256]{2,1,0:T(8,128)(2,1)} copy(bf16[16,64,256]{2,0,1:T(8,128)(2,1)} %bitcast.21) | data formatting | bytes 1048576
  68.0 0.0 copy-done.2
  68.0 0.7 copy.35
  (3 shorter events, 0.0 us)
Async XLA Ops:
  0.6 2.3 %copy-start.1 = (bf16[1024,128]{1,0:T(8,128)(2,1)S(1)}, bf16[1024,128]{1,0:T(8,128)(2,1)}, u32[]{:S(2)}) copy-start(bf16[1024,128]{1,0:T(8,128)(2,1)} %param.30) | copy-start | bytes 786436
  1.4 0.7 %copy-start.3 = (bf16[256,32]{0,1:T(8,128)(2,1)S(1)}, bf16[256,32]{0,1:T(8,128)(2,1)}, u32[]{:S(2)}) copy-start(bf16[256,32]{0,1:T(8,128)(2,1)} %param.28) | copy-start | bytes 49156
  2.9 1.0 %copy-start = (bf16[16,64,256]{2,1,0:T(8,128)(2,1)S(1)}, bf16[16,64,256]{2,1,0:T(8,128)(2,1)}, u32[]{:S(2)}) copy-start(bf16[16,64,256]{2,1,0:T(8,128)(2,1)} %param.17) | copy-start | bytes 1572868
  65.9 2.0 %copy-start.2 = (bf16[8,64,128]{2,1,0:T(8,128)(2,1)S(1)}, bf16[8,64,128]{2,1,0:T(8,128)(2,1)}, u32[]{:S(2)}) copy-start(bf16[8,64,128]{2,1,0:T(8,128)(2,1)} %get-tuple-element.13) | copy-start | bytes 393220

commit v2 on v1

--- a/solution.py
+++ b/solution.py
@@ -189,6 +189,18 @@
         updated = (after.astype(F32) + mm(hidden, wn_v[...])).astype(BF16)
         ycol[c] = updated
         n3[c] = layer_norm(updated.astype(F32)).astype(BF16)
+
+        @pl.loop(1, n)
+        def _(k):
+            dst = lax.rem(me + k, n)
+            remote(
+                ycol.at[c, pl.ds(pl.multiple_of(dst * shard_rows, shard_rows), shard_rows)],
+                msa_out.at[me * OWNED + c],
+                o_send,
+                o_recv,
+                at(dst),
+            ).start()
+
         return carry
 
     lax.fori_loop(0, OWNED, column, 0)
@@ -252,17 +264,6 @@
         z, _, block = line_block(k)
         got(block, ry_recv.at[z])
         pass_on(block, rc_recv.at[1, z], c_pair)
-
-    @pl.loop(1, n)
-    def _(k):
-        dst = lax.rem(me + k, n)
-        remote(
-            ycol.at[:, pl.ds(pl.multiple_of(dst * shard_rows, shard_rows), shard_rows)],
-            msa_out.at[pl.ds(me * OWNED, OWNED)],
-            o_send,
-            o_recv,
-            at(dst),
-        ).start()
 
     home = pltpu.make_async_copy(
         ycol.at[:, my_rows], msa_out.at[pl.ds(me * OWNED, OWNED)], own_sem

time: 69 us -> 64.7 us (0.938)
  the two profiles are of different devices: /device:TPU:15 before, /device:TPU:23 now
where the time goes in v2:
time: 64.7 us; the launch traced here: 64.3 us
  Pallas kernels  56.6 us (87%)
  local copies, waits for them, and re-layouts  7.06 us (11%)
  between operations  0.68 us (1%)
    pallas_call x1, Pallas kernels, per_device(): pl.pallas_call(functools.partial(kernel, n, res_n), out_shape=(jax.ShapeD...  56.6 us
    unnamed x12, local copies, waits for them, and re-layouts  4.65 us

profile of v2, /device:TPU:23, one launch (start us, length us, event | category | flops | bytes accessed | tf_op | source)
XLA Modules:
  0.0 64.3 jit_solution(10151901241479147477)
XLA Ops:
  0.6 0.0 copy-start.1
  0.6 0.8 %reshape.27 = bf16[8,4,1,256]{3,1,0,2:T(4,128)(2,1)S(1)} reshape(bf16[32,256]{1,0:T(8,128)(2,1)} %bitcast.25) | data formatting | bytes 32768 | tf_op jit(solution)/shard_map/reshape | solution.py:373
  1.4 0.0 copy-start.3
  1.5 0.7 %reshape.28.w2 = bf16[128,256]{1,0:T(8,128)(2,1)} reshape(bf16[4,8,4,256]{3,2,1,0:T(4,128)(2,1)S(1)} %broadcast_in_dim.8) | data formatting | bytes 131072 | tf_op jit(solution)/shard_map/reshape | solution.py:376
  2.1 0.1 copy-done.3
  2.2 0.7 %copy.27.w1 = bf16[256,128]{1,0:T(8,128)(2,1)} copy(bf16[256,128]{0,1:T(8,128)(2,1)S(1)} %bitcast.22) | data formatting | bytes 131072 | tf_op jit(solution)/shard_map/tile | solution.py:372
  2.9 0.0 copy-done.1
  2.9 0.0 copy-start
  2.9 0.2 copy.26
  3.1 0.7 %copy.33 = bf16[64,8,2,128]{3,1,2,0:T(8,128)(2,1)} copy(bf16[64,8,2,128]{3,2,1,0:T(2,128)(2,1)S(1)} %bitcast.20) | data formatting | bytes 524288
  3.9 0.1 copy-done
  4.0 1.1 %copy.32 = bf16[16,64,256]{2,0,1:T(8,128)(2,1)} copy(bf16[16,64,256]{2,1,0:T(8,128)(2,1)S(1)} %copy-done) | data formatting | bytes 1048576 | tf_op args[0]
  5.0 56.6 %shard_map.176 = (bf16[64,16,256]{2,1,0:T(8,128)(2,1)}, bf16[8,64,128]{2,1,0:T(8,128)(2,1)}) custom-call(bf16[64,16,256]{2,1,0:T(8,128)(2,1)} %bitcast.18, bf16[8,64,128]{2,1,0:T(8,128)(2,1)} %pair_ref.1, s32[1,256]{1,0:T(1,128)} %bitcast.26, s32[128]{0:T(128)} %keep_ref.1, bf16[256,256]{1,0:T(8,128)(2,1)} %wq.1, bf16[256,256]{1,0:T(8,128)(2,1)} %wk.1, ...), custom_call_target="tpu_custom_call" | custom-call | tf_op jit(solution)/shard_map/pallas_call | solution.py:384
  61.6 0.0 copy-start.2
  61.6 2.0 %copy.28 = bf16[16,64,256]{2,1,0:T(8,128)(2,1)} copy(bf16[16,64,256]{2,0,1:T(8,128)(2,1)} %bitcast.21) | data formatting | bytes 1048576
  63.7 0.0 copy-done.2
  63.7 0.7 %copy.35 = bf16[8,64,128]{2,1,0:T(8,128)(2,1)} copy(bf16[8,64,128]{2,1,0:T(8,128)(2,1)S(1)} %copy-done.2) | data formatting | bytes 262144
  (3 shorter events, 0.0 us)
Async XLA Ops:
  0.6 2.3 %copy-start.1 = (bf16[1024,128]{1,0:T(8,128)(2,1)S(1)}, bf16[1024,128]{1,0:T(8,128)(2,1)}, u32[]{:S(2)}) copy-start(bf16[1024,128]{1,0:T(8,128)(2,1)} %param.30) | copy-start | bytes 786436
  1.4 0.7 %copy-start.3 = (bf16[256,32]{0,1:T(8,128)(2,1)S(1)}, bf16[256,32]{0,1:T(8,128)(2,1)}, u32[]{:S(2)}) copy-start(bf16[256,32]{0,1:T(8,128)(2,1)} %param.28) | copy-start | bytes 49156
  2.9 1.0 %copy-start = (bf16[16,64,256]{2,1,0:T(8,128)(2,1)S(1)}, bf16[16,64,256]{2,1,0:T(8,128)(2,1)}, u32[]{:S(2)}) copy-start(bf16[16,64,256]{2,1,0:T(8,128)(2,1)} %param.17) | copy-start | bytes 1572868
  61.6 2.0 %copy-start.2 = (bf16[8,64,128]{2,1,0:T(8,128)(2,1)S(1)}, bf16[8,64,128]{2,1,0:T(8,128)(2,1)}, u32[]{:S(2)}) copy-start(bf16[8,64,128]{2,1,0:T(8,128)(2,1)} %get-tuple-element.13) | copy-start | bytes 393220
